TPU v7x, 128 devices: a whole 4x4x4 slice. The times are simulated.
128 devices in a mesh: section: 16 (over z_lo, y, core), ep: 8 (over z_hi, x).
Axes of the slice: x: 4, y: 4, z: 4 (z_hi: 2, z_lo: 2; z = z_hi * 2 + z_lo), core: 2. Of those that a mesh axis runs over, the one named last changes fastest.
Arguments:
- fwd_input: bfloat16 [16, 1024, 3584], P('section', 'ep'), may hold values from -6 to 6
- bwd_input: bfloat16 [16, 1024, 3584], P('section', 'ep'), may hold values from -6 to 6
- bwd_grad: bfloat16 [16, 1024, 3584], P('section', 'ep'), may hold values from -6 to 6
- fwd_ids: int32 [16, 1024, 2], P('section', 'ep'), may hold values from 0 to 7, all different within a row; in each aligned block of 128 rows (0 to 127, 128 to 255, ...) at most 48 rows name the same one
- bwd_ids: int32 [16, 1024, 2], P('section', 'ep'), may hold values from 0 to 7, all different within a row; in each aligned block of 128 rows (0 to 127, 128 to 255, ...) at most 48 rows name the same one
- norm_gain: float32 [16, 3584], P('section'), may hold values from 0.5 to 1.5
- router: bfloat16 [16, 3584, 8], P('section'), may hold values from -0.09375 to 0.09375
- gate_w: bfloat16 [16, 8, 3584, 1024], P('section', 'ep'), may hold values from -0.09375 to 0.09375
- up_w: bfloat16 [16, 8, 3584, 1024], P('section', 'ep'), may hold values from -0.09375 to 0.09375
- down_w: bfloat16 [16, 8, 1024, 3584], P('section', 'ep'), may hold values from -0.1875 to 0.1875
Outputs:
- fwd_next: bfloat16 [16, 1024, 3584], P('section', 'ep')
- bwd_prev: bfloat16 [16, 1024, 3584], P('section', 'ep')
Inputs may be any that keep to these rules, and one draw needn't show every extreme that they name: `fwd_ids`: each token names 2 different experts of 0 to 7; among the 128 tokens of one index of ep in one section no expert is named more than 48 times, a bound that some block reaches. `bwd_ids`: each token names 2 different experts of 0 to 7; among the 128 tokens of one index of ep in one section no expert is named more than 48 times, a bound that some block reaches.
All inputs are finite; a program needn't handle non-finite values.
Results may differ from a plain program's by a relative error of at most 0.0035.
Values may be sent and summed in bfloat16 or wider, within the bound.
A program may use at most 128 MiB of HBM per device.

v0:
```python
import jax
import jax.numpy as jnp
from jax import lax
from jax.experimental import pallas as pl
from jax.experimental.pallas import tpu as pltpu
from jax.sharding import PartitionSpec as P

NORM_EPSILON = 1e-06
ROUTE_SCALE = 2.5

D = 3584
F = 1024
T = 128
E = 8
CAP = 48
S = E * CAP
NEP = 8
NSEC = 16
MODES = (0, 1, 0)
BACK_ORDER = ((0, 1), (1, 0), (1, -1), (1, 1), (0, 2), (1, 2), (0, -1))
OUT_ORDER = ((0, 1), (1, 0), (0, -1), (1, 1), (0, 2), (1, -1), (1, 2))

BACK_CHUNKS = 7
BACK_WIDTH = D // BACK_CHUNKS
OUT_CHUNKS = 4
OUT_WIDTH = D // OUT_CHUNKS

HAND_PARTS = 4

MESH = pl.DeviceIdType.MESH
F32 = jnp.float32
BF16 = jnp.bfloat16


def dot(a, b):
    return jnp.dot(a, b, preferred_element_type=F32)


def dot_t(a, b):
    return lax.dot_general(a, b, (((1,), (1,)), ((), ())), preferred_element_type=F32)


def cols(i, width):
    return pl.ds(pl.multiple_of(i * width, 128), width)


def block(i):
    return pl.ds(pl.multiple_of(i * CAP, 16), CAP)


def kernel(
    ids_f, ids_b, gain, router, hf_hbm, hb_hbm, g_hbm, gate_hbm, up_hbm, down_hbm,
    outf_hbm, outb_hbm,
    gate, up, down, hf, hb, g,
    send, recv, raw, retb, retf, norm, pmat, qmat, scale, wmat_b, wmat_f,
    dact, dab, act, dacc, dots, dotr, u, stage_f, stage_b, inv, small, idx, share,
    wsem, isem, xsem_s, xsem_r, rsem_s, rsem_r, dsem_s, dsem_r, bsem_s, bsem_r, tsem_s, tsem_r,
    fsem_s, fsem_r, pf_s, pf_r, pb_s, pb_r,
):
    sec = lax.axis_index("section")
    me = lax.axis_index("ep")
    mx, mz = lax.rem(me, 4), me // 4
    side = 1 - 2 * lax.rem(sec, 2)

    def at_place(dz, dx):
        return lax.rem(mz + dz, 2) * 4 + lax.rem(mx + dx + 4, 4)

    back_peers = [at_place(dz, side * dx) for dz, dx in BACK_ORDER]
    out_peers = [at_place(dz, side * dx) for dz, dx in OUT_ORDER]
    across = at_place(1, 0)
    onward, source = at_place(0, side), at_place(0, -side)
    ahead, behind = lax.rem(sec + 1, NSEC), lax.rem(sec + NSEC - 1, NSEC)

    barrier = pltpu.get_barrier_semaphore()
    for e in back_peers:
        pl.semaphore_signal(barrier, 1, device_id={"ep": e}, device_id_type=MESH)
    for s in (ahead, behind):
        pl.semaphore_signal(barrier, 1, device_id={"section": s}, device_id_type=MESH)

    loads = [
        pltpu.make_async_copy(src, dst, isem.at[i])
        for i, (src, dst) in enumerate(((hb_hbm, hb), (g_hbm, g), (hf_hbm, hf)))
    ]
    weights = [
        pltpu.make_async_copy(src, dst, wsem.at[i])
        for i, (src, dst) in enumerate(((down_hbm, down), (gate_hbm, gate), (up_hbm, up)))
    ]
    for c in (loads[1], loads[0], loads[2]):
        c.start()

    def remote(src, dst, ssem, rsem, e):
        return pltpu.make_async_remote_copy(
            src_ref=src, dst_ref=dst, send_sem=ssem, recv_sem=rsem,
            device_id={"ep": e}, device_id_type=MESH,
        )

    row16 = lax.broadcasted_iota(jnp.int32, (16, T), 0)
    slot48 = lax.broadcasted_iota(jnp.int32, (CAP, T), 0).astype(F32)
    eye48 = (
        lax.broadcasted_iota(jnp.int32, (CAP, T), 0) == lax.broadcasted_iota(jnp.int32, (CAP, T), 1)
    ).astype(F32)
    earlier = (
        lax.broadcasted_iota(jnp.int32, (T, T), 0) < lax.broadcasted_iota(jnp.int32, (T, T), 1)
    ).astype(BF16)

    def places(ids0, ids1, order):
        eid = jnp.full((16, T), -1, jnp.int32)
        for k, e in enumerate(order):
            eid = jnp.where(row16 == k, e, eid)
        named = ((ids0 == eid) | (ids1 == eid)).astype(F32)
        rank = dot(named.astype(BF16), earlier)
        return eid, [
            jnp.where((slot48 == rank[k:k + 1, :]) & (named[k:k + 1, :] > 0.5), 1.0, 0.0)
            for k in range(len(order))
        ]

    def weighted(placed, ids0, ids1, eid, w0, w1):
        per = jnp.where(ids0 == eid, w0, 0.0) + jnp.where(ids1 == eid, w1, 0.0)
        return [p * per[k:k + 1, :] for k, p in enumerate(placed)]

    def pack(flow, half, owner, ids0, ids1, order, rows, w=None):
        eid, placed = places(ids0, ids1, order)
        qmat[...] = jnp.concatenate(placed, axis=0).astype(BF16)
        if w is not None:
            per = jnp.concatenate(weighted(placed, ids0, ids1, eid, w[0], w[1]), axis=0)
            scale[...] = jnp.broadcast_to(jnp.sum(per, axis=1, keepdims=True), (4 * CAP, 128))

        def step(i, c):
            at = cols(i, 512)
            packed = dot(qmat[...], rows[:, at])
            if w is not None:
                packed = scale[:, 0:1] * packed
            packed = packed.astype(BF16)
            recv[flow, block(owner), at] = packed[0:CAP]
            send[flow, half * 3 * CAP:(half + 1) * 3 * CAP, at] = packed[CAP:4 * CAP]
            return c

        lax.fori_loop(0, D // 512, step, 0)

    def launch(flow, half, owner, order):
        for k, e in enumerate(order[1:]):
            remote(
                send.at[flow, pl.ds((half * 3 + k) * CAP, CAP)], recv.at[flow, block(owner)],
                dsem_s.at[flow], dsem_r.at[flow], e,
            ).start()

    def packed_all(flow):
        part = pl.ds(0, 6 * CAP)
        return remote(
            send.at[flow, part], recv.at[flow, part], dsem_s.at[flow], dsem_r.at[flow], across
        )

    def forward_raw(flow, rows, e):
        return remote(rows, raw.at[flow], rsem_s.at[flow], rsem_r.at[flow], e)

    def normalize(rows, into, keep):
        def step(i, c):
            at = pl.ds(pl.multiple_of(i * 16, 16), 16)
            x = rows[at, :].astype(F32)
            r = lax.rsqrt(jnp.mean(x * x, axis=1, keepdims=True) + NORM_EPSILON)
            if keep is not None:
                keep[at, :] = jnp.broadcast_to(r, (16, 128))
            into[at, :] = (x * r * gain[...]).astype(BF16)
            return c

        lax.fori_loop(0, T // 16, step, 0)

    expert8 = lax.broadcasted_iota(jnp.int32, (E, T), 0)

    def route(ids, rows):
        scores = jax.nn.sigmoid(dot_t(router[...], rows[...]))
        s0 = jnp.sum(jnp.where(expert8 == ids[0:1, :], scores, 0.0), axis=0, keepdims=True)
        s1 = jnp.sum(jnp.where(expert8 == ids[1:2, :], scores, 0.0), axis=0, keepdims=True)
        total = s0 + s1
        return scores, s0 / total, s1 / total

    by_plane = [me, at_place(0, 1), at_place(0, 3), at_place(0, 2)]
    by_column = [me, at_place(0, -side), across, at_place(1, -side)]
    relayed = [me, at_place(0, side), across, at_place(1, side)]
    target = [onward if m else across for m in MODES]
    origin = [source if m else across for m in MODES]
    direct = [by_column if m else by_plane for m in MODES]
    relay = [relayed if m else by_plane for m in MODES]
    if MODES[2] == 0:
        relay[2] = [me, at_place(0, -1), at_place(0, 1), at_place(0, 2)]

    ids_copies = [
        remote(ids_b, idx.at[0], xsem_s.at[0], xsem_r.at[0], target[0]),
        remote(ids_b, idx.at[1], xsem_s.at[1], xsem_r.at[1], target[1]),
        remote(ids_f, idx.at[2], xsem_s.at[2], xsem_r.at[2], target[2]),
    ]
    share_copy = remote(share.at[0], share.at[1], xsem_s.at[3], xsem_r.at[3], target[1])

    pl.semaphore_wait(barrier, 9)
    raw_g = forward_raw(1, g, target[1])
    raw_b = forward_raw(0, norm.at[0], target[0])
    raw_f = forward_raw(2, norm.at[1], target[2])
    loads[1].wait()
    raw_g.start()
    for c in ids_copies:
        c.start()
    loads[0].wait()
    normalize(hb, norm.at[0], inv)
    raw_b.start()
    b0, b1 = ids_b[0:1, :], ids_b[1:2, :]
    f0, f1 = ids_f[0:1, :], ids_f[1:2, :]
    pack(0, 0, me, b0, b1, direct[0], norm.at[0])
    launch(0, 0, me, direct[0])
    for c in weights:
        c.start()

    scores, w0, w1 = route(ids_b, norm.at[0])
    small[0] = scores
    small[1] = jnp.broadcast_to(w0, (E, T))
    small[2] = jnp.broadcast_to(w1, (E, T))
    share[0, 0:1, :] = ROUTE_SCALE * w0
    share[0, 1:2, :] = ROUTE_SCALE * w1
    share_copy.start()
    pack(1, 0, me, b0, b1, direct[1], g, (ROUTE_SCALE * w0, ROUTE_SCALE * w1))
    launch(1, 0, me, direct[1])

    loads[2].wait()
    normalize(hf, norm.at[1], None)

    ids_copies[1].wait_recv()
    share_copy.wait_recv()
    raw_g.wait_recv()
    pack(
        1, 1, origin[1], idx[1, 0:1, :], idx[1, 1:2, :], relay[1], raw.at[1],
        (share[1, 0:1, :], share[1, 1:2, :]),
    )
    launch(1, 1, origin[1], relay[1])

    pack(2, 0, me, f0, f1, direct[2], norm.at[1])
    _, w0, w1 = route(ids_f, norm.at[1])
    eid, placed = places(f0, f1, list(range(E)))
    w = jnp.transpose(jnp.concatenate(
        weighted(placed, f0, f1, eid, ROUTE_SCALE * w0, ROUTE_SCALE * w1), axis=0
    ))
    hi = w.astype(BF16)
    wmat_f[0:T, :] = hi
    wmat_f[T:2 * T, :] = (w - hi.astype(F32)).astype(BF16)
    _, placed = places(b0, b1, list(range(E)))
    placed = jnp.concatenate(placed, axis=0)
    pmat[...] = placed.astype(BF16)
    wmat_b[...] = jnp.transpose(placed).astype(BF16)

    ids_copies[0].wait_recv()
    raw_b.wait_recv()
    pack(0, 1, origin[0], idx[0, 0:1, :], idx[0, 1:2, :], relay[0], raw.at[0])
    launch(0, 1, origin[0], relay[0])

    raw_f.start()
    launch(2, 0, me, direct[2])

    for c in weights:
        c.wait()
    packed_all(1).wait_recv()

    def d_act(i, c):
        at = cols(i, 256)
        dact[:, at] = dot_t(recv[1], down[pl.ds(pl.multiple_of(i * 256, 256), 256), :])
        return c

    lax.fori_loop(0, F // 256, d_act, 0)
    packed_all(0).wait_recv()
    dacc[...] = jnp.zeros_like(dacc)

    def hidden_grad(i, c):
        at = cols(i, 256)
        a = dot(recv[0], gate[:, at])
        b = dot(recv[0], up[:, at])
        da = dact[:, at]
        sg = jax.nn.sigmoid(a)
        silu = a * sg
        live = silu * b * da
        dacc[...] += live[:, 0:128] + live[:, 128:256]
        dab[:, at] = (da * b * sg * (1.0 + a * (1.0 - sg))).astype(BF16)
        dab[:, pl.ds(pl.multiple_of(F + i * 256, 128), 256)] = (da * silu).astype(BF16)
        return c

    lax.fori_loop(0, F // 256, hidden_grad, 0)

    ids_copies[2].wait_recv()
    raw_f.wait_recv()
    pack(2, 1, origin[2], idx[2, 0:1, :], idx[2, 1:2, :], relay[2], raw.at[2])
    launch(2, 1, origin[2], relay[2])

    for e in range(E):
        column = jnp.sum(dacc[e * CAP:(e + 1) * CAP, :], axis=1, keepdims=True)
        dots[e] = jnp.broadcast_to(jnp.sum(column * eye48, axis=0, keepdims=True), (E, T))
    for e in back_peers:
        remote(dots.at[e], dotr.at[me], tsem_s, tsem_r, e).start()
    dotr[me] = dots[me]

    def d_rows(i, c):
        at = pl.ds(pl.multiple_of(i * 256, 256), 256)
        recv[0, :, cols(i, 256)] = (
            dot_t(dab[:, 0:F], gate[at, :]) + dot_t(dab[:, F:2 * F], up[at, :])
        ).astype(BF16)
        return c

    for chunk in range(BACK_CHUNKS):
        each = BACK_WIDTH // 256
        lax.fori_loop(chunk * each, (chunk + 1) * each, d_rows, 0)
        at = pl.ds(chunk * BACK_WIDTH, BACK_WIDTH)
        for e in back_peers:
            remote(
                recv.at[0, block(e), at], retb.at[block(me), at],
                bsem_s.at[chunk], bsem_r.at[chunk], e,
            ).start()
        retb[block(me), at] = recv[0, block(me), at]

    packed_all(2).wait_recv()

    def hidden(i, c):
        at = cols(i, 256)
        a = dot(recv[2], gate[:, at])
        b = dot(recv[2], up[:, at])
        act[:, at] = (a * jax.nn.sigmoid(a) * b).astype(BF16)
        return c

    lax.fori_loop(0, F // 256, hidden, 0)

    for chunk in range(OUT_CHUNKS):
        at = pl.ds(chunk * OUT_WIDTH, OUT_WIDTH)
        recv[1, :, at] = dot(act[...], down[:, at]).astype(BF16)
        for e in out_peers:
            remote(
                recv.at[1, block(e), at], retf.at[block(me), at],
                fsem_s.at[chunk], fsem_r.at[chunk], e,
            ).start()
        retf[block(me), at] = recv[1, block(me), at]

    seven = pl.ds(0, 7 * CAP)
    all_dots = remote(dots.at[pl.ds(0, 7)], dotr.at[pl.ds(0, 7)], tsem_s, tsem_r, across)
    all_dots.wait_recv()
    scores = small[0]
    w0, w1 = small[1, 0:1, :], small[2, 0:1, :]
    d0 = jnp.zeros((1, T), F32)
    d1 = jnp.zeros((1, T), F32)
    for e in range(E):
        column = jnp.sum(dotr[e, 0:1, :] * eye48, axis=1, keepdims=True)
        value = jnp.sum(
            pmat[e * CAP:(e + 1) * CAP, :].astype(F32) * column, axis=0, keepdims=True
        )
        d0 = d0 + jnp.where(b0 == e, value, 0.0)
        d1 = d1 + jnp.where(b1 == e, value, 0.0)
    mean = d0 + d1
    d_logits = (
        jnp.where(expert8 == b0, d0 - w0 * mean, 0.0) + jnp.where(expert8 == b1, d1 - w1 * mean, 0.0)
    ) * (1.0 - scores)
    d_logits = jnp.transpose(
        jnp.concatenate([d_logits, jnp.zeros((T - E, T), F32)], axis=0)
    )[:, 0:E].astype(BF16)

    def all_back(chunk):
        at = pl.ds(chunk * BACK_WIDTH, BACK_WIDTH)
        return remote(
            recv.at[0, seven, at], retb.at[seven, at], bsem_s.at[chunk], bsem_r.at[chunk], across
        )

    def all_out(chunk):
        at = pl.ds(chunk * OUT_WIDTH, OUT_WIDTH)
        return remote(
            recv.at[1, seven, at], retf.at[seven, at], fsem_s.at[chunk], fsem_r.at[chunk], across
        )

    total_uh = jnp.zeros((T, 1), F32)
    for chunk in range(BACK_CHUNKS):
        all_back(chunk).wait_recv()
        for part in range(1):
            at = pl.ds(chunk * BACK_WIDTH + part * BACK_WIDTH, BACK_WIDTH)
            d_normed = dot(wmat_b[...], retb[:, at]) + dot(d_logits, router[:, at])
            scaled = gain[:, at] * d_normed
            u[:, at] = scaled
            total_uh = total_uh + jnp.sum(scaled * hb[:, at].astype(F32), axis=1, keepdims=True)
    r = inv[:, 0:1]
    pull = r * r * r * total_uh * (1.0 / D)

    def next_copy(at, out, stage, ssem, rsem, target):
        return pltpu.make_async_remote_copy(
            src_ref=stage.at[:, at], dst_ref=out.at[:, at], send_sem=ssem, recv_sem=rsem,
            device_id={"section": target}, device_id_type=MESH,
        )

    for chunk in range(OUT_CHUNKS):
        at = pl.ds(chunk * OUT_WIDTH, OUT_WIDTH)
        stage_b[:, at] = (
            g[:, at].astype(F32) + r * u[:, at] - hb[:, at].astype(F32) * pull
        ).astype(BF16)
        next_copy(at, outb_hbm, stage_b, pb_s, pb_r, behind).start()

    for chunk in range(OUT_CHUNKS):
        at = pl.ds(chunk * OUT_WIDTH, OUT_WIDTH)
        all_out(chunk).wait_recv()
        both = dot(wmat_f[...], retf[:, at])
        stage_f[:, at] = (hf[:, at].astype(F32) + (both[0:T] + both[T:2 * T])).astype(BF16)
        next_copy(at, outf_hbm, stage_f, pf_s, pf_r, ahead).start()

    for c in [*ids_copies, share_copy, raw_g, raw_b, raw_f, all_dots]:
        c.wait_send()
    for flow in range(3):
        packed_all(flow).wait_send()
    for chunk in range(BACK_CHUNKS):
        all_back(chunk).wait_send()
    for chunk in range(OUT_CHUNKS):
        all_out(chunk).wait_send()
    every = pl.ds(0, D)
    next_copy(every, outb_hbm, stage_b, pb_s, pb_r, behind).wait()
    next_copy(every, outf_hbm, stage_f, pf_s, pf_r, ahead).wait()


def hand_over(a_in, b_in, a_out, b_out, held, isem, osem):
    rows = T // HAND_PARTS
    pairs = [
        (src.at[pl.ds(i * rows, rows)], dst.at[pl.ds(i * rows, rows)])
        for i in range(HAND_PARTS)
        for src, dst in ((a_in, a_out), (b_in, b_out))
    ]
    ins = [pltpu.make_async_copy(s, held.at[i], isem.at[i]) for i, (s, _) in enumerate(pairs)]
    outs = [pltpu.make_async_copy(held.at[i], d, osem.at[i]) for i, (_, d) in enumerate(pairs)]
    for c in ins:
        c.start()
    for i, c in enumerate(outs):
        ins[i].wait()
        c.start()
    for c in outs:
        c.wait()


def local(
    fwd_input, bwd_input, bwd_grad, fwd_ids, bwd_ids, norm_gain, router, gate_w, up_w, down_w
):
    vmem = pl.BlockSpec(memory_space=pltpu.VMEM)
    hbm = pl.BlockSpec(memory_space=pl.ANY)
    dma = pltpu.SemaphoreType.DMA
    out = jax.ShapeDtypeStruct((T, D), BF16)
    fwd_next, bwd_prev = pl.pallas_call(
        kernel,
        out_shape=(out, out),
        in_specs=[vmem] * 4 + [hbm] * 6,
        out_specs=(hbm, hbm),
        scratch_shapes=[
            pltpu.VMEM((D, F), BF16), pltpu.VMEM((D, F), BF16), pltpu.VMEM((F, D), BF16),
            pltpu.VMEM((T, D), BF16), pltpu.VMEM((T, D), BF16), pltpu.VMEM((T, D), BF16),
            pltpu.VMEM((3, 6 * CAP, D), BF16), pltpu.VMEM((3, S, D), BF16), pltpu.VMEM((3, T, D), BF16),
            pltpu.VMEM((S, D), BF16), pltpu.VMEM((S, D), BF16), pltpu.VMEM((2, T, D), BF16),
            pltpu.VMEM((S, T), BF16), pltpu.VMEM((4 * CAP, T), BF16), pltpu.VMEM((4 * CAP, 128), F32),
            pltpu.VMEM((T, S), BF16), pltpu.VMEM((2 * T, S), BF16),
            pltpu.VMEM((S, F), F32), pltpu.VMEM((S, 2 * F), BF16), pltpu.VMEM((S, F), BF16),
            pltpu.VMEM((S, 128), F32), pltpu.VMEM((E, E, T), F32), pltpu.VMEM((E, E, T), F32),
            pltpu.VMEM((T, D), F32), pltpu.VMEM((T, D), BF16), pltpu.VMEM((T, D), BF16),
            pltpu.VMEM((T, 128), F32), pltpu.VMEM((3, E, T), F32),
            pltpu.VMEM((3, 2, T), jnp.int32), pltpu.VMEM((2, E, T), F32),
            dma((3,)), dma((3,)), dma((4,)), dma((4,)), dma((3,)), dma((3,)), dma((3,)), dma((3,)),
            dma((BACK_CHUNKS,)), dma((BACK_CHUNKS,)), dma, dma,
            dma((OUT_CHUNKS,)), dma((OUT_CHUNKS,)), dma, dma, dma, dma,
        ],
        compiler_params=pltpu.CompilerParams(
            collective_id=0, has_side_effects=True, vmem_limit_bytes=67043328
        ),
    )(
        fwd_ids[0].T, bwd_ids[0].T, norm_gain, router[0].T,
        fwd_input[0], bwd_input[0], bwd_grad[0], gate_w[0, 0], up_w[0, 0], down_w[0, 0],
    )
    parts = 2 * HAND_PARTS
    fwd_next, bwd_prev = pl.pallas_call(
        hand_over,
        out_shape=(out, out),
        in_specs=[hbm, hbm],
        out_specs=(hbm, hbm),
        scratch_shapes=[
            pltpu.VMEM((parts, T // HAND_PARTS, D), BF16), dma((parts,)), dma((parts,)),
        ],
    )(fwd_next, bwd_prev)
    return (fwd_next[None], bwd_prev[None])


def solution(mesh):
    placed = (
        P("section", "ep", None),
        P("section", "ep", None),
        P("section", "ep", None),
        P("section", "ep", None),
        P("section", "ep", None),
        P("section", None),
        P("section", None, None),
        P("section", "ep", None, None),
        P("section", "ep", None, None),
        P("section", "ep", None, None),
    )
    return jax.shard_map(
        local,
        mesh=mesh,
        in_specs=placed,
        out_specs=(P("section", "ep", None), P("section", "ep", None)),
        check_vma=False,
    )
```

profile of v0, /device:TPU:32, one launch (start us, length us, event | category | flops | bytes accessed | tf_op | source)
XLA Modules:
  0.0 172.9 jit_solution(9073173501409585943)
XLA Ops:
  0.6 169.7 %shard_map.113 = (bf16[128,3584]{1,0:T(8,128)(2,1)}, bf16[128,3584]{1,0:T(8,128)(2,1)}) custom-call(s32[2,128]{1,0:T(2,128)} %bitcast.24, s32[2,128]{1,0:T(2,128)} %bitcast.25, f32[1,3584]{1,0:T(1,128)} %gain.1, bf16[8,3584]{1,0:T(8,128)(2,1)} %bitcast.23, bf16[128,3584]{1,0:T(8,128)(2,1)} %bitcast.20, bf16[128,3584]{1,0:T(8,128)(2,1)} %bitcast.21, ...), custom_call_target="tpu_custom_call" | custom-call | tf_op jit(solution)/shard_map/pallas_call | solution.py:439
  170.3 2.4 %shard_map.114 = (bf16[128,3584]{1,0:T(8,128)(2,1)}, bf16[128,3584]{1,0:T(8,128)(2,1)}) custom-call(bf16[128,3584]{1,0:T(8,128)(2,1)} %get-tuple-element.6.a_in, bf16[128,3584]{1,0:T(8,128)(2,1)} %get-tuple-element.7.b_in), custom_call_target="tpu_custom_call" | custom-call | tf_op jit(solution)/shard_map/pallas_call | solution.py:468
where the time goes:
time: 173 us
  Pallas kernels  172 us (99%)
    pallas_call x1, Pallas kernels, local(): pl.pallas_call(kernel, out_shape=(out, out), in_specs=[vmem] * 4 + [hbm]...  170 us

commit v1 on v0

--- a/solution.py
+++ b/solution.py
@@ -17,7 +17,7 @@
 NEP = 8
 NSEC = 16
 MODES = (0, 1, 0)
-BACK_ORDER = ((0, 1), (1, 0), (1, -1), (1, 1), (0, 2), (1, 2), (0, -1))
+BACK_ORDER = ((0, 2), (1, 0), (1, -1), (1, 1), (0, 1), (1, 2), (0, -1))
 OUT_ORDER = ((0, 1), (1, 0), (0, -1), (1, 1), (0, 2), (1, -1), (1, 2))
 
 BACK_CHUNKS = 7

time: 173 us -> 172 us (level); the launches traced: 173 us -> 170 us
  Pallas kernels: 172 us -> 169 us
    pallas_call x1, Pallas kernels: 170 us -> 167 us  [local(): pl.pallas_call(kernel, out_shape=(out, out), in_specs=[vmem] * 4 + [hbm]...]
where the time goes in v1:
time: 172 us; the launch traced here: 170 us
  Pallas kernels  169 us (98%)
    pallas_call x1, Pallas kernels, local(): pl.pallas_call(kernel, out_shape=(out, out), in_specs=[vmem] * 4 + [hbm]...  167 us

profile of v1, /device:TPU:32, one launch (start us, length us, event | category | flops | bytes accessed | tf_op | source)
XLA Modules:
  0.0 169.9 jit_solution(8790844992251042312)
XLA Ops:
  0.6 166.7 %shard_map.113 = (bf16[128,3584]{1,0:T(8,128)(2,1)}, bf16[128,3584]{1,0:T(8,128)(2,1)}) custom-call(s32[2,128]{1,0:T(2,128)} %bitcast.24, s32[2,128]{1,0:T(2,128)} %bitcast.25, f32[1,3584]{1,0:T(1,128)} %gain.1, bf16[8,3584]{1,0:T(8,128)(2,1)} %bitcast.23, bf16[128,3584]{1,0:T(8,128)(2,1)} %bitcast.20, bf16[128,3584]{1,0:T(8,128)(2,1)} %bitcast.21, ...), custom_call_target="tpu_custom_call" | custom-call | tf_op jit(solution)/shard_map/pallas_call | solution.py:439
  167.3 2.4 %shard_map.114 = (bf16[128,3584]{1,0:T(8,128)(2,1)}, bf16[128,3584]{1,0:T(8,128)(2,1)}) custom-call(bf16[128,3584]{1,0:T(8,128)(2,1)} %get-tuple-element.6.a_in, bf16[128,3584]{1,0:T(8,128)(2,1)} %get-tuple-element.7.b_in), custom_call_target="tpu_custom_call" | custom-call | tf_op jit(solution)/shard_map/pallas_call | solution.py:468

commit v2 on v1

--- a/solution.py
+++ b/solution.py
@@ -174,7 +174,7 @@
         total = s0 + s1
         return scores, s0 / total, s1 / total
 
-    by_plane = [me, at_place(0, 1), at_place(0, 3), at_place(0, 2)]
+    by_plane = [me, at_place(0, side), at_place(0, -side), at_place(0, 2)]
     by_column = [me, at_place(0, -side), across, at_place(1, -side)]
     relayed = [me, at_place(0, side), across, at_place(1, side)]
     target = [onward if m else across for m in MODES]
@@ -232,6 +232,13 @@
     launch(1, 1, origin[1], relay[1])
 
     pack(2, 0, me, f0, f1, direct[2], norm.at[1])
+    ids_copies[0].wait_recv()
+    raw_b.wait_recv()
+    pack(0, 1, origin[0], idx[0, 0:1, :], idx[0, 1:2, :], relay[0], raw.at[0])
+    launch(0, 1, origin[0], relay[0])
+
+    raw_f.start()
+    launch(2, 0, me, direct[2])
     _, w0, w1 = route(ids_f, norm.at[1])
     eid, placed = places(f0, f1, list(range(E)))
     w = jnp.transpose(jnp.concatenate(
@@ -245,13 +252,6 @@
     pmat[...] = placed.astype(BF16)
     wmat_b[...] = jnp.transpose(placed).astype(BF16)
 
-    ids_copies[0].wait_recv()
-    raw_b.wait_recv()
-    pack(0, 1, origin[0], idx[0, 0:1, :], idx[0, 1:2, :], relay[0], raw.at[0])
-    launch(0, 1, origin[0], relay[0])
-
-    raw_f.start()
-    launch(2, 0, me, direct[2])
 
     for c in weights:
         c.wait()

time: 172 us -> 171 us (level); the launches traced: 170 us -> 171 us
  no operation moved by 1% of the time
where the time goes in v2:
time: 171 us
  Pallas kernels  170 us (99%)
    pallas_call x1, Pallas kernels, local(): pl.pallas_call(kernel, out_shape=(out, out), in_specs=[vmem] * 4 + [hbm]...  168 us

profile of v2, /device:TPU:32, one launch (start us, length us, event | category | flops | bytes accessed | tf_op | source)
XLA Modules:
  0.0 171.1 jit_solution(15719373354659473317)
XLA Ops:
  0.6 167.9 %shard_map.113 = (bf16[128,3584]{1,0:T(8,128)(2,1)}, bf16[128,3584]{1,0:T(8,128)(2,1)}) custom-call(s32[2,128]{1,0:T(2,128)} %bitcast.24, s32[2,128]{1,0:T(2,128)} %bitcast.25, f32[1,3584]{1,0:T(1,128)} %gain.1, bf16[8,3584]{1,0:T(8,128)(2,1)} %bitcast.23, bf16[128,3584]{1,0:T(8,128)(2,1)} %bitcast.20, bf16[128,3584]{1,0:T(8,128)(2,1)} %bitcast.21, ...), custom_call_target="tpu_custom_call" | custom-call | tf_op jit(solution)/shard_map/pallas_call | solution.py:439
  168.5 2.4 %shard_map.114 = (bf16[128,3584]{1,0:T(8,128)(2,1)}, bf16[128,3584]{1,0:T(8,128)(2,1)}) custom-call(bf16[128,3584]{1,0:T(8,128)(2,1)} %get-tuple-element.6.a_in, bf16[128,3584]{1,0:T(8,128)(2,1)} %get-tuple-element.7.b_in), custom_call_target="tpu_custom_call" | custom-call | tf_op jit(solution)/shard_map/pallas_call | solution.py:468
